TPU v7x, 512 devices: a whole 4x8x8 slice. The times are simulated.
512 devices in a mesh: expert: 8 (over x, core), shard: 64 (over y, z).
Axes of the slice: x: 4, y: 8, z: 8, core: 2. Of those that a mesh axis runs over, the one named last changes fastest.
Arguments:
- tokens: bfloat16 [384, 4096], P('shard', 'expert'), may hold values from -6 to 6
- expert_ids: int32 [384, 2], P('shard'), may hold values from 0 to 7, all different within a row; in each aligned block of 6 rows (0 to 5, 6 to 11, ...) at most 3 rows name the same one
- gates: float32 [384, 2], P('shard'), may hold values from 0.1 to 1
- gate_proj: bfloat16 [8, 4096, 8192], P('expert', None, 'shard'), may hold values from -0.09375 to 0.09375
- up_proj: bfloat16 [8, 4096, 8192], P('expert', None, 'shard'), may hold values from -0.09375 to 0.09375
- down_proj_t: bfloat16 [8, 4096, 8192], P('expert', 'shard'), may hold values from -0.0625 to 0.0625
Outputs:
- mixed: bfloat16 [384, 4096], P('shard', 'expert')
Inputs may be any that keep to these rules, and one draw needn't show every extreme that they name: `expert_ids`: each token names two different experts; among the 6 tokens of one aligned block no expert is named more than 3 times, and in every draw some expert is named exactly 3 times in some block.
All inputs are finite; a program needn't handle non-finite values.
Results may differ from a plain program's by a relative error of at most 0.0085.
Values may be sent and summed in bfloat16 or wider, within the bound.
A program may use at most 64 MiB of HBM per device.

v0:
```python
import jax
import jax.numpy as jnp
from jax import lax
from jax.sharding import Mesh
from jax.sharding import PartitionSpec as P

SHARD = ("shard_0", "shard_1")


def in_order(parts, dim):
    parts = jnp.moveaxis(parts, 0, dim)
    lengths = parts.shape
    return parts.reshape(*lengths[:dim], lengths[dim] * lengths[dim + 1], *lengths[dim + 2 :])


def all_blocks(value, axes, turns):
    parts = value[None]
    for k in turns:
        parts = lax.all_gather(parts, axes[k], axis=0, tiled=True)
    held = [lax.axis_size(axes[k]) for k in reversed(turns)]
    parts = parts.reshape(*held, *value.shape)
    turned = sorted(range(len(turns)), key=lambda place: turns[len(turns) - 1 - place])
    return parts.transpose(*turned, *range(len(turns), parts.ndim)).reshape(-1, *value.shape)


def gathered_by_axis(value, axes, turns, dim):
    return in_order(all_blocks(value, axes, turns), dim)


def in_blocks(value, dim, length):
    before, after = (value.shape[:dim], value.shape[dim + 1 :])
    return jnp.moveaxis(value.reshape(*before, length, -1, *after), dim, 0)


def sum_at_owner(value, axis, dim):
    length = lax.axis_size(axis)
    parts = lax.all_to_all(in_blocks(value, dim, length), axis, 0, 0, tiled=True)
    return jnp.sum(parts.astype(jnp.float32), axis=0)


def shards(tokens, expert_ids, gates, gate_proj, up_proj, down_proj_t):
    experts = lax.axis_size("expert")
    tok_count = tokens.shape[0]
    capacity = min(tok_count, 4 * tok_count // experts)
    expert_range = jnp.arange(experts, dtype=jnp.int32)
    matches = expert_ids[:, :, None] == expert_range[None, None, :]
    routed = jnp.sum(matches.astype(jnp.int32), axis=1)
    weight = jnp.sum(gates[:, :, None] * matches.astype(jnp.float32), axis=1)
    slot_rank = jnp.cumsum(routed, axis=0) - routed
    slot_range = jnp.arange(capacity, dtype=jnp.int32)
    selector = (slot_rank.T[:, None, :] == slot_range[None, :, None]) & (routed.T[:, None, :] > 0)
    selector_bf = selector.astype(jnp.bfloat16)
    outgoing = jnp.einsum(
        "ect,td->ecd", selector_bf, tokens, preferred_element_type=jnp.float32
    ).astype(jnp.bfloat16)
    arrived = lax.all_to_all(outgoing, "expert", split_axis=0, concat_axis=2, tiled=True)
    own_rows = arrived[0]
    gate_local = gate_proj[0]
    up_local = up_proj[0]
    down_local = down_proj_t[0]
    piece = gathered_by_axis(own_rows, SHARD, (0, 1), 0)
    gate_out = jnp.dot(piece, gate_local, preferred_element_type=jnp.float32)
    up_out = jnp.dot(piece, up_local, preferred_element_type=jnp.float32)
    hidden = (jax.nn.silu(gate_out) * up_out).astype(jnp.bfloat16)
    down_rows = lax.all_to_all(down_local, SHARD, split_axis=1, concat_axis=0, tiled=True)
    expert_out = sum_at_owner(
        lax.dot_general(
            hidden, down_rows, (((1,), (1,)), ((), ())), preferred_element_type=jnp.float32
        ).astype(jnp.bfloat16),
        SHARD,
        0,
    ).astype(jnp.bfloat16)
    gathered_out = lax.all_to_all(expert_out, "expert", split_axis=1, concat_axis=0, tiled=True)
    combiner = (
        (selector.astype(jnp.float32) * weight.T[:, None, :])
        .reshape(experts * capacity, tok_count)
        .T
    )
    mixed_sum = jnp.dot(combiner, gathered_out.astype(jnp.float32), precision=lax.Precision.HIGHEST)
    return mixed_sum.astype(jnp.bfloat16)


def solution(mesh):
    split = Mesh(mesh.devices.reshape(mesh.shape["expert"], 8, 8), ("expert", "shard_0", "shard_1"))
    placed = (
        P(SHARD, "expert"),
        P(SHARD, None),
        P(SHARD, None),
        P("expert", None, SHARD),
        P("expert", None, SHARD),
        P("expert", SHARD, None),
    )
    return jax.shard_map(
        shards, mesh=split, in_specs=placed, out_specs=P(SHARD, "expert"), check_vma=False
    )
```

profile of v0, /device:TPU:1, one launch (start us, length us, event | category | flops | bytes accessed | tf_op | source)
XLA Modules:
  0.0 199.7 jit_solution(2765780398806376705)
XLA Ops:
  6.5 0.0 copy-start
  6.5 0.0 copy-start.1
  6.5 0.0 all-gather.2.cloned.1.call-start
  6.5 0.9 copy.27
  7.5 0.1 convert_reduce_fusion
  7.6 0.9 convolution_convert_fusion.1
  8.5 13.9 %all_to_all.58 = bf16[8,3,512]{2,1,0:T(4,128)(2,1)S(1)} all-to-all(bf16[8,3,512]{2,1,0:T(4,128)(2,1)S(1)} %copy.30), channel_id=1, replica_groups=mesh['expert'=8,'shard_0'=8,'shard_1'=8] {'expert'}, dimensions={0} | all-to-all | bytes 49152 | tf_op jit(solution)/shard_map/all_to_all | solution.py:56
  22.4 18.7 %all_gather.6 = bf16[8,3,4096]{2,1,0:T(4,128)(2,1)S(1)} all-gather(bf16[1,3,4096]{2,1,0:T(4,128)(2,1)S(1)} %bitcast.43), channel_id=1, replica_groups=mesh['expert'=8,'shard_0'=8,'shard_1'=8] {'shard_0'}, dimensions={0}, use_global_device_ids=true | all-gather | bytes 221184 | tf_op jit(solution)/shard_map/all_gather | solution.py:19
  41.2 0.8 copy.31
  42.0 0.0 all-gather.2.cloned.1.call-update
  42.0 0.0 copy-done.1
  42.0 0.3 copy.36
  42.3 1.7 copy.33
  44.0 13.0 %all-to-all-start.1 = ((bf16[64,64,128]{2,0,1:T(8,128)(2,1)}), bf16[64,64,128]{2,0,1:T(8,128)(2,1)}, u32[]{:S(2)}, u32[]{:S(2)}) async-start(bf16[64,64,128]{2,0,1:T(8,128)(2,1)} %copy.33), calls=%async_computation.1 | async-start | bytes 2097152 | tf_op jit(solution)/shard_map/all_to_all | solution.py:65
  57.0 47.5 %all-gather.2.cloned.1.call-done = bf16[64,3,4096]{2,0,1:T(8,128)(2,1)} async-done(((bf16[8,3,4096]{2,0,1:T(8,128)(2,1)}), bf16[64,3,4096]{2,0,1:T(8,128)(2,1)}) %all-gather.2.cloned.1.call-update) | async-done | bytes 1572880 | tf_op jit(solution)/shard_map/all_gather | solution.py:19
  104.5 4.1 %copy.32 = bf16[8,8,3,4096]{3,2,1,0:T(4,128)(2,1)} copy(bf16[8,8,3,4096]{3,0,1,2:T(8,128)(2,1)} %bitcast.41) | data formatting | bytes 3145728 | tf_op jit(solution)/shard_map/transpose | solution.py:23
  108.7 3.1 %reshape_reshape.3 = bf16[192,4096]{1,0:T(8,128)(2,1)S(1)} reshape(bf16[8,8,3,4096]{3,2,1,0:T(4,128)(2,1)} %copy.32) | data formatting | bytes 3145728 | tf_op jit(solution)/shard_map/reshape;reshape | solution.py:13
  111.8 1.8 fusion.4
  113.6 0.0 all-to-all-done.1
  113.6 0.0 copy-done
  113.6 3.4 %convolution_convert_fusion = bf16[192,4096]{1,0:T(8,128)(2,1)} fusion(bf16[4096,128]{1,0:T(8,128)(2,1)} %bitcast.12, bf16[192,4096]{1,0:T(8,128)(2,1)S(1)} %reshape_reshape.3, bf16[1,4096,128]{2,1,0:T(8,128)(2,1)S(1)} %copy-done, f32[192,128]{1,0:T(8,128)S(1)} %fusion.4), kind=kOutput, calls=%fused_computation | convolution fusion | flops 403587072 | bytes 5341184 | tf_op jit(solution)/shard_map/dot_general | solution.py:67
  117.0 4.1 %reshape.21 = bf16[64,3,4096]{2,1,0:T(4,128)(2,1)} reshape(bf16[192,4096]{1,0:T(8,128)(2,1)} %convolution_convert_fusion) | data formatting | bytes 3145728 | tf_op jit(solution)/shard_map/reshape | solution.py:32
  121.1 0.0 copy-start.2
  121.1 8.9 %all-to-all-start.2 = ((bf16[64,3,4096]{2,1,0:T(4,128)(2,1)}), bf16[64,3,4096]{2,1,0:T(4,128)(2,1)S(1)}, u32[]{:S(2)}, u32[]{:S(2)}) async-start(bf16[64,3,4096]{2,1,0:T(4,128)(2,1)} %reshape.21), calls=%async_computation.2 | async-start | bytes 4194304 | tf_op jit(solution)/shard_map/all_to_all | solution.py:37
  130.0 0.0 copy-done.2
  130.0 0.1 copy.28
  130.1 46.0 %all-to-all-done.2 = bf16[64,3,4096]{2,1,0:T(4,128)(2,1)S(1)} async-done(((bf16[64,3,4096]{2,1,0:T(4,128)(2,1)}), bf16[64,3,4096]{2,1,0:T(4,128)(2,1)S(1)}, u32[]{:S(2)}, u32[]{:S(2)}) %all-to-all-start.2) | async-done | bytes 1572896 | tf_op jit(solution)/shard_map/all_to_all | solution.py:37
  176.1 1.5 reduce_sum.32
  177.6 9.7 %all-to-all-start.3 = ((bf16[3,8,512]{2,0,1:T(4,128)(2,1)}), bf16[3,8,512]{2,0,1:T(4,128)(2,1)S(1)}, u32[]{:S(2)}, u32[]{:S(2)}) async-start(bf16[3,8,512]{2,0,1:T(4,128)(2,1)} %bitcast.13), calls=%async_computation.3 | async-start | bytes 65536 | tf_op jit(solution)/shard_map/all_to_all | solution.py:73
  187.4 0.1 select_reduce_fusion
  187.4 4.6 %all-to-all-done.3 = bf16[3,8,512]{2,0,1:T(4,128)(2,1)S(1)} async-done(((bf16[3,8,512]{2,0,1:T(4,128)(2,1)}), bf16[3,8,512]{2,0,1:T(4,128)(2,1)S(1)}, u32[]{:S(2)}, u32[]{:S(2)}) %all-to-all-start.3) | async-done | bytes 24608 | tf_op jit(solution)/shard_map/all_to_all | solution.py:73
  192.1 0.8 fusion.1
  (4 shorter events, 0.1 us)
Async XLA Ops:
  6.5 107.1 %copy-start = (bf16[1,4096,128]{2,1,0:T(8,128)(2,1)S(1)}, bf16[1,4096,128]{2,1,0:T(8,128)(2,1)}, u32[]{:S(2)}) copy-start(bf16[1,4096,128]{2,1,0:T(8,128)(2,1)} %param.10) | copy-start | bytes 3145732
  6.5 35.5 %copy-start.1 = (bf16[1,64,8192]{2,1,0:T(8,128)(2,1)S(1)}, bf16[1,64,8192]{2,1,0:T(8,128)(2,1)}, u32[]{:S(2)}) copy-start(bf16[1,64,8192]{2,1,0:T(8,128)(2,1)} %param.11) | copy-start | bytes 3145732
  6.5 98.0 %all-gather.2.cloned.1.call-start = ((), (), s32[]{:S(2)}) async-start(), calls=%async_computation.4 | async-start | bytes 1769472 | tf_op jit(solution)/shard_map/all_gather | solution.py:19
  44.0 69.6 %all-to-all-start.1 = ((bf16[64,64,128]{2,0,1:T(8,128)(2,1)}), bf16[64,64,128]{2,0,1:T(8,128)(2,1)}, u32[]{:S(2)}, u32[]{:S(2)}) async-start(bf16[64,64,128]{2,0,1:T(8,128)(2,1)} %copy.33), calls=%async_computation.1 | async-start | bytes 2097152 | tf_op jit(solution)/shard_map/all_to_all | solution.py:65
  121.1 8.9 %copy-start.2 = (f32[6,2]{0,1:T(2,128)S(1)}, f32[6,2]{0,1:T(2,128)}, u32[]{:S(2)}) copy-start(f32[6,2]{0,1:T(2,128)} %param.8) | copy-start | bytes 148
  121.1 55.0 %all-to-all-start.2 = ((bf16[64,3,4096]{2,1,0:T(4,128)(2,1)}), bf16[64,3,4096]{2,1,0:T(4,128)(2,1)S(1)}, u32[]{:S(2)}, u32[]{:S(2)}) async-start(bf16[64,3,4096]{2,1,0:T(4,128)(2,1)} %reshape.21), calls=%async_computation.2 | async-start | bytes 4194304 | tf_op jit(solution)/shard_map/all_to_all | solution.py:37
  177.6 14.4 %all-to-all-start.3 = ((bf16[3,8,512]{2,0,1:T(4,128)(2,1)}), bf16[3,8,512]{2,0,1:T(4,128)(2,1)S(1)}, u32[]{:S(2)}, u32[]{:S(2)}) async-start(bf16[3,8,512]{2,0,1:T(4,128)(2,1)} %bitcast.13), calls=%async_computation.3 | async-start | bytes 65536 | tf_op jit(solution)/shard_map/all_to_all | solution.py:73
Sparse Core Ops, SparseCore 0:
  42.1 62.3 all-gather.1
where the time goes:
time: 203 us; the launch traced here: 200 us
  waiting for transfers between devices  98.1 us (48%)
  blocking collectives  32.7 us (16%)
  starting transfers between devices  31.6 us (16%)
  local copies, waits for them, and re-layouts  15.1 us (7%)
  between operations  13.5 us (7%)
  matrix products  6.91 us (3%)
    all_gather x1, waiting for transfers between devices, all_blocks(): parts = lax.all_gather(parts, axes[k], axis=0, tiled=True)  47.5 us
    all_to_all x1, waiting for transfers between devices, sum_at_owner(): lax.all_to_all(in_blocks(value, dim, length), axis, 0, 0, tiled=True)  46 us
    all_gather x1, blocking collectives, all_blocks(): parts = lax.all_gather(parts, axes[k], axis=0, tiled=True)  18.7 us
    all_to_all x1, blocking collectives, shards(): lax.all_to_all(outgoing, 'expert', split_axis=0, concat_axis=2, tiled=True)  13.9 us
    all_to_all x1, starting transfers between devices, shards(): lax.all_to_all(down_local, SHARD, split_axis=1, concat_axis=0, tiled=True)  13 us
    all_to_all x1, starting transfers between devices, shards(): lax.all_to_all(expert_out, 'expert', split_axis=1, concat_axis=0, tiled=T...  9.73 us
    all_to_all x1, starting transfers between devices, sum_at_owner(): lax.all_to_all(in_blocks(value, dim, length), axis, 0, 0, tiled=True)  8.89 us
    all_to_all x1, waiting for transfers between devices, shards(): lax.all_to_all(expert_out, 'expert', split_axis=1, concat_axis=0, tiled=T...  4.63 us
  transfers between devices with their start and end apart: 4, of which 3 were waited for; matrix products, arithmetic and copies ran while one was open for 6% of the time, Pallas kernels for 0%

commit v1 on v0

v1 whole, which is shorter than its diff:
```python
import functools

import jax
import jax.numpy as jnp
from jax import lax
from jax.experimental import pallas as pl
from jax.experimental.pallas import tpu as pltpu
from jax.sharding import Mesh
from jax.sharding import PartitionSpec as P

SHARD = ("shard_0", "shard_1")
MESH = pl.DeviceIdType.MESH
NARROW = ("shard_1", "shard_0")
WIDE = ("shard_0", "shard_1")
CHUNKS = 4


def loop(count, body):
    lax.fori_loop(0, count, lambda i, c: (body(i), c)[1], 0)


def kernel(
    n, cap, half, hidden_units,
    msg_ref, comb_ref, gate_hbm, up_hbm, down_hbm, out_ref,
    toks, sel, rows, part, hid, acc, give, got, back, gate_w, up_w, down_w,
    load_sem, a1_send, a1_recv, a2_send, a2_recv, a3_send, a3_recv,
    c1_send, c1_recv, c2_send, c2_recv, e1_send, e1_recv, e2_send, e2_recv,
):
    e = lax.axis_index("expert")
    y = lax.axis_index("shard_0")
    z = lax.axis_index("shard_1")
    nar = (z, y)
    wid = (y, z)
    top = n // 2
    line = n * cap
    total = n * line
    hrows = total // 2
    groups = line // 8
    per = n // CHUNKS if n >= CHUNKS else 1
    chunks = n // per

    def plus(a, b):
        return lax.rem(a + b + n, n)

    loads = [
        pltpu.make_async_copy(gate_hbm, gate_w, load_sem.at[0]),
        pltpu.make_async_copy(up_hbm, up_w, load_sem.at[1]),
        pltpu.make_async_copy(down_hbm, down_w.at[0], load_sem.at[2]),
        pltpu.make_async_copy(down_hbm, down_w.at[1], load_sem.at[3]),
    ]
    for copy in loads:
        copy.start()

    barrier = pltpu.get_barrier_semaphore()
    for axis, own in (("expert", e), ("shard_0", y), ("shard_1", z)):
        for d in range(1, n):
            pl.semaphore_signal(
                barrier, inc=1, device_id={axis: plus(own, d)}, device_id_type=MESH
            )
    pl.semaphore_wait(barrier, 3 * (n - 1))

    def a1(h, d):
        return pltpu.make_async_remote_copy(
            src_ref=msg_ref.at[h],
            dst_ref=toks.at[h, nar[h]],
            send_sem=a1_send.at[h, d],
            recv_sem=a1_recv.at[h, d],
            device_id={NARROW[h]: plus(nar[h], -d)},
            device_id_type=MESH,
        )

    for d in range(1, n):
        for h in range(2):
            a1(h, d).start()
    for h in range(2):
        toks[h, nar[h]] = msg_ref[h]

    def a2(h, d):
        return pltpu.make_async_remote_copy(
            src_ref=sel.at[h, plus(e, -d)],
            dst_ref=rows.at[h, wid[h], d],
            send_sem=a2_send.at[h, d],
            recv_sem=a2_recv.at[h, d],
            device_id={"expert": plus(e, -d)},
            device_id_type=MESH,
        )

    lanes = 8 * n
    row_of = lax.broadcasted_iota(jnp.int32, (line, 128), 0)
    lane_of = lax.broadcasted_iota(jnp.int32, (line, 128), 1)
    same_block = (row_of // cap) == (lane_of // 8)
    rank_of = (row_of % cap + 1).astype(jnp.float32)
    for h in range(2):
        for d in range(1, n):
            a1(h, d).wait_recv()
        codes = jnp.zeros((8, 128), jnp.float32)
        for b in range(n):
            codes = codes + toks[h, b, :, half:].astype(jnp.float32)
        feats = toks[h, :, :, :half].reshape(lanes, half)
        for k in range(n):
            hit = same_block & (codes[k : k + 1, :] == rank_of)
            pick = jnp.where(hit, 1.0, 0.0).astype(jnp.bfloat16)[:, :lanes]
            found = jnp.dot(pick, feats, preferred_element_type=jnp.float32)
            sel[h, k] = found.reshape(groups, 8, half).astype(jnp.bfloat16)
        for d in range(1, n):
            a2(h, d).start()
        rows[h, wid[h], 0] = sel[h, e]

    def a3(h, way, k, j):
        step = 1 if way == 0 else -1
        unit = rows.at[h, plus(wid[h], -step * (k - 1)), pl.ds(j * per, per)]
        return pltpu.make_async_remote_copy(
            src_ref=unit,
            dst_ref=unit,
            send_sem=a3_send.at[h, way, k - 1, j],
            recv_sem=a3_recv.at[h, way, k - 1, j],
            device_id={WIDE[h]: plus(wid[h], step)},
            device_id_type=MESH,
        )

    def split(way, k, j, count):
        return k < top or (j < count // 2) == (way == 0)

    for j in range(chunks):
        for h in range(2):
            for d in range(j * per, (j + 1) * per):
                if d > 0:
                    a2(h, d).wait_recv()
            for way in range(2):
                if split(way, 1, j, chunks):
                    a3(h, way, 1, j).start()
    for k in range(1, top + 1):
        for j in range(chunks):
            for h in range(2):
                for way in range(2):
                    if split(way, k, j, chunks):
                        a3(h, way, k, j).wait_recv()
                    if k < top and split(way, k + 1, j, chunks):
                        a3(h, way, k + 1, j).start()

    for copy in loads:
        copy.wait()
    for h in range(2):
        part[h] = jnp.zeros((total, 2 * hidden_units), jnp.float32)

        def project(d, h=h):
            at = pl.multiple_of(plus(e, d) * (2 * half) + h * half, half)
            lhs = rows[h, :, d].reshape(total, half)
            rhs = jnp.concatenate([gate_w[pl.ds(at, half), :], up_w[pl.ds(at, half), :]], axis=1)
            part[h] += jnp.dot(lhs, rhs, preferred_element_type=jnp.float32)

        loop(n, project)
    for a in range(n):
        for b in range(n):
            to, at = a * line + b * cap, b * line + a * cap
            part[1, to : to + cap, :] += part[0, at : at + cap, :]
    both = part[1]
    gated = both[:, :hidden_units]
    hidden = ((gated / (1.0 + jnp.exp(-gated))) * both[:, hidden_units:]).astype(jnp.bfloat16)
    for h in range(2):
        hid[h, wid[h], 0] = hidden[h * hrows : (h + 1) * hrows, :]

    def c1(h, d):
        return pltpu.make_async_remote_copy(
            src_ref=hid.at[h, wid[h], 0],
            dst_ref=hid.at[h, wid[h], d],
            send_sem=c1_send.at[h, d],
            recv_sem=c1_recv.at[h, d],
            device_id={NARROW[h]: plus(nar[h], -d)},
            device_id_type=MESH,
        )

    order = [0]
    for d in range(1, top):
        order += [d, n - d]
    order.append(top)
    for d in order[1:]:
        for h in range(2):
            c1(h, d).start()

    def c2(h, way, k, d):
        step = 1 if way == 0 else -1
        unit = hid.at[h, plus(wid[h], -step * (k - 1)), d]
        return pltpu.make_async_remote_copy(
            src_ref=unit,
            dst_ref=unit,
            send_sem=c2_send.at[h, way, k - 1, d],
            recv_sem=c2_recv.at[h, way, k - 1, d],
            device_id={WIDE[h]: plus(wid[h], step)},
            device_id_type=MESH,
        )

    acc[...] = jnp.zeros_like(acc)

    def use(h, src, pair):
        lhs, rhs = [], []
        for d in pair:
            other = plus(nar[h], d)
            unit = src * n + other if h == 0 else other * n + src
            at = pl.multiple_of(unit * hidden_units, hidden_units)
            lhs.append(hid[h, src, d])
            rhs.append(down_w[:, :, pl.ds(at, hidden_units)].reshape(128, hidden_units))
        acc[h] += lax.dot_general(
            jnp.concatenate(lhs, axis=1),
            jnp.concatenate(rhs, axis=1),
            (((1,), (1,)), ((), ())),
            preferred_element_type=jnp.float32,
        )

    for j, d in enumerate(order):
        for h in range(2):
            if d > 0:
                c1(h, d).wait_recv()
            for way in range(2):
                if split(way, 1, j, n):
                    c2(h, way, 1, d).start()
    for k in range(1, top + 1):
        for i in range(n // 2):
            pair = order[2 * i : 2 * i + 2]
            for h in range(2):
                for way in range(2):
                    for j in (2 * i, 2 * i + 1):
                        if split(way, k, j, n):
                            c2(h, way, k, order[j]).wait_recv()
                        if k < top and split(way, k + 1, j, n):
                            c2(h, way, k + 1, order[j]).start()
            for h in range(2):
                if k == 1:
                    use(h, wid[h], pair)
                else:
                    use(h, plus(wid[h], -(k - 1)), pair)
                    use(h, plus(wid[h], k - 1), pair)
    for i in range(n // 2):
        for h in range(2):
            use(h, plus(wid[h], top), order[2 * i : 2 * i + 2])

    for a in range(n):
        for b in range(n):
            at = (a % top) * line + b * cap
            give[a, b] = acc[a // top, at : at + cap, :].astype(jnp.bfloat16)

    def e1(d):
        return pltpu.make_async_remote_copy(
            src_ref=give.at[plus(z, -d)],
            dst_ref=got.at[z],
            send_sem=e1_send.at[d],
            recv_sem=e1_recv.at[d],
            device_id={"shard_1": plus(z, -d)},
            device_id_type=MESH,
        )

    for d in range(1, n):
        e1(d).start()
    got[z] = give[z]
    for d in range(1, n):
        e1(d).wait_recv()

    def e2(b, src):
        return pltpu.make_async_remote_copy(
            src_ref=got.at[:, b],
            dst_ref=back.at[src],
            send_sem=e2_send.at[b],
            recv_sem=e2_recv.at[src],
            device_id={"expert": y, "shard_0": b},
            device_id_type=MESH,
        )

    for b in range(n):
        here = (e == y) & (y == b)

        @pl.when(jnp.logical_not(here))
        def _(b=b):
            e2(b, e).start()

        @pl.when(here)
        def _(b=b):
            back[e] = got[:, b]

    for src in range(n):

        @pl.when(jnp.logical_not((src == e) & (y == e)))
        def _(src=src):
            e2(0, src).wait_recv()

    coefs = comb_ref[...]
    low = lax.broadcasted_iota(jnp.int32, (cap, 128), 1) < 64
    sums = [jnp.zeros((8, 128), jnp.float32) for _ in range(n // 2)]
    for src in range(n):
        for m in range(n // 2):
            value = jnp.where(
                low,
                back[src, 2 * m].astype(jnp.float32),
                back[src, 2 * m + 1].astype(jnp.float32),
            )
            for s in range(cap):
                at = src * cap + s
                sums[m] = sums[m] + coefs[:, at : at + 1] * value[s : s + 1, :]
    for m in range(n // 2):
        out_ref[:, m * 128 : (m + 1) * 128] = sums[m][: out_ref.shape[0], :].astype(jnp.bfloat16)

    for h in range(2):
        for d in range(1, n):
            a1(h, d).wait_send()
            a2(h, d).wait_send()
            c1(h, d).wait_send()
        for way in range(2):
            for k in range(1, top + 1):
                for j in range(chunks):
                    if split(way, k, j, chunks):
                        a3(h, way, k, j).wait_send()
                for j in range(n):
                    if split(way, k, j, n):
                        c2(h, way, k, order[j]).wait_send()
    for d in range(1, n):
        e1(d).wait_send()
    for b in range(n):

        @pl.when(jnp.logical_not((e == y) & (y == b)))
        def _(b=b):
            e2(b, e).wait_send()


def shards(n, tokens, expert_ids, gates, gate_proj, up_proj, down_proj_t):
    tok_count, feats = tokens.shape
    half = feats // 2
    hidden_units = gate_proj.shape[2]
    out_feats = down_proj_t.shape[1]
    cap = min(tok_count, 4 * tok_count // n)
    y, z = lax.axis_index("shard_0"), lax.axis_index("shard_1")
    expert_range = jnp.arange(n, dtype=jnp.int32)
    matches = expert_ids[:, :, None] == expert_range[None, None, :]
    routed = jnp.sum(matches.astype(jnp.int32), axis=1)
    weight = jnp.sum(gates[:, :, None] * matches.astype(jnp.float32), axis=1)
    rank = jnp.cumsum(routed, axis=0) - routed
    code = jnp.where(routed > 0, rank + 1, 0)
    slot = jnp.arange(cap, dtype=jnp.int32)
    picked = jnp.where(code[:, :, None] == slot[None, None, :] + 1, weight[:, :, None], 0.0)
    comb = jnp.pad(
        picked.reshape(tok_count, n * cap), ((0, 8 - tok_count), (0, 128 - n * cap))
    )
    lane = jnp.arange(128, dtype=jnp.int32)
    tok = jnp.arange(tok_count, dtype=jnp.int32)
    msgs = []
    for h, at in enumerate((z, y)):
        place = lane[None, :] == at * 8 + tok[:, None]
        meta = jnp.sum(jnp.where(place[:, None, :], code[:, :, None], 0), axis=0)
        meta = jnp.pad(meta, ((0, 8 - n), (0, 0))).astype(jnp.bfloat16)
        body = jnp.pad(tokens[:, h * half : (h + 1) * half], ((0, 8 - tok_count), (0, 0)))
        msgs.append(jnp.concatenate([body, meta], axis=1))
    msg = jnp.stack(msgs)

    line = n * cap
    total = n * line
    bf16 = jnp.bfloat16
    per = n // CHUNKS if n >= CHUNKS else 1
    dma = pltpu.SemaphoreType.DMA
    vmem, hbm = pltpu.VMEM, pl.ANY
    return pl.pallas_call(
        functools.partial(kernel, n, cap, half, hidden_units),
        out_shape=jax.ShapeDtypeStruct((tok_count, feats), bf16),
        in_specs=[
            pl.BlockSpec(memory_space=vmem),
            pl.BlockSpec(memory_space=vmem),
            pl.BlockSpec(memory_space=hbm),
            pl.BlockSpec(memory_space=hbm),
            pl.BlockSpec(memory_space=hbm),
        ],
        out_specs=pl.BlockSpec(memory_space=vmem),
        scratch_shapes=[
            vmem((2, n, 8, half + 128), bf16),
            vmem((2, n, line // 8, 8, half), bf16),
            vmem((2, n, n, line // 8, 8, half), bf16),
            vmem((2, total, 2 * hidden_units), jnp.float32),
            vmem((2, n, n, total // 2, hidden_units), bf16),
            vmem((2, total // 2, 128), jnp.float32),
            vmem((n, n, cap, 128), bf16),
            vmem((n, n, cap, 128), bf16),
            vmem((n, n, cap, 128), bf16),
            vmem(gate_proj.shape[1:], bf16),
            vmem(up_proj.shape[1:], bf16),
            vmem((2, out_feats, down_proj_t.shape[2]), bf16),
            dma((4,)),
            dma((2, n)), dma((2, n)),
            dma((2, n)), dma((2, n)),
            dma((2, 2, n // 2, n // per)), dma((2, 2, n // 2, n // per)),
            dma((2, n)), dma((2, n)),
            dma((2, 2, n // 2, n)), dma((2, 2, n // 2, n)),
            dma((n,)), dma((n,)),
            dma((n,)), dma((n,)),
        ],
        compiler_params=pltpu.CompilerParams(collective_id=0, has_side_effects=True),
        name="experts",
    )(msg, comb, gate_proj[0], up_proj[0], down_proj_t[0])


def solution(mesh):
    n = mesh.shape["expert"]
    split = Mesh(mesh.devices.reshape(n, n, n), ("expert", "shard_0", "shard_1"))
    placed = (
        P(SHARD, "expert"),
        P(SHARD, None),
        P(SHARD, None),
        P("expert", None, SHARD),
        P("expert", None, SHARD),
        P("expert", SHARD, None),
    )
    return jax.shard_map(
        functools.partial(shards, n),
        mesh=split,
        in_specs=placed,
        out_specs=P(SHARD, "expert"),
        check_vma=False,
    )
```

time: 203 us -> 85 us (0.42); the launches traced: 200 us -> 84.2 us
  waiting for transfers between devices: 98.1 us -> 0 us
  Pallas kernels: 0 us -> 78.6 us
  blocking collectives: 32.7 us -> 0 us
  starting transfers between devices: 31.6 us -> 0 us
  between operations: 13.5 us -> 0.05 us
  local copies, waits for them, and re-layouts: 15.1 us -> 4.43 us
  matrix products: 6.91 us -> 0 us
    pallas_call x0 -> x1, Pallas kernels: none -> 78.6 us  [shards(): pl.pallas_call(functools.partial(kernel, n, cap, half, hidden_units), out...]
    all_to_all x3 -> x0, waiting for transfers between devices: 50.6 us -> none  [the longest x1 46 us: sum_at_owner(): lax.all_to_all(in_blocks(value, dim, length), axis, 0, 0, tiled=True)]
    all_gather x1 -> x0, waiting for transfers between devices: 47.5 us -> none  [all_blocks(): parts = lax.all_gather(parts, axes[k], axis=0, tiled=True)]
    all_to_all x3 -> x0, starting transfers between devices: 31.6 us -> none  [the longest x1 13 us: shards(): lax.all_to_all(down_local, SHARD, split_axis=1, concat_axis=0, tiled=True)]
    all_gather x1 -> x0, blocking collectives: 18.7 us -> none  [all_blocks(): parts = lax.all_gather(parts, axes[k], axis=0, tiled=True)]
    all_to_all x1 -> x0, blocking collectives: 13.9 us -> none  [shards(): lax.all_to_all(outgoing, 'expert', split_axis=0, concat_axis=2, tiled=True)]
    dot_general x4 -> x0, matrix products: 6.91 us -> none  [the longest x1 3.43 us: shards(): lax.dot_general(hidden, down_rows, (((1,), (1,)), ((), ())), preferred_el...]
    transpose x1 -> x0, local copies, waits for them, and re-layouts: 4.11 us -> none  [all_blocks(): parts.transpose(*turned, *range(len(turns), parts.ndim))]
  transfers between devices with their start and end apart: 4 -> 0, of which waited for: 3 -> 0; matrix products, arithmetic and copies ran while one was open for 6% -> 0% of each run, Pallas kernels for 0% -> 0%
where the time goes in v1:
time: 85 us; the launch traced here: 84.2 us
  Pallas kernels  78.6 us (92%)
  local copies, waits for them, and re-layouts  4.43 us (5%)
  other arithmetic  1.08 us (1%)
    pallas_call x1, Pallas kernels, shards(): pl.pallas_call(functools.partial(kernel, n, cap, half, hidden_units), out...  78.6 us
    unnamed x7, local copies, waits for them, and re-layouts  3.44 us

profile of v1, /device:TPU:1, one launch (start us, length us, event | category | flops | bytes accessed | tf_op | source)
XLA Modules:
  0.0 84.2 jit_solution(5178467304697592055)
XLA Ops:
  0.0 0.8 copy.11
  0.8 0.1 convert_reduce_fusion
  0.9 0.1 iota_compare_fusion.2
  1.0 0.1 iota_compare_fusion.3
  1.1 0.1 select_reduce_fusion.1
  1.1 0.0 copy-start
  1.2 0.7 copy-done
  1.8 0.6 pad_maximum_fusion.msg_ref
  2.5 0.1 eq.76
  2.5 0.0 copy-start.1
  2.5 0.1 eq.77
  2.6 0.6 copy-done.1
  3.2 0.1 copy.12
  3.3 0.1 select_reduce_fusion.2
  3.4 0.1 broadcast_in_dim.63
  3.5 0.1 broadcast_in_dim.64
  3.6 0.1 eq.79
  3.6 0.6 pad.13.comb_ref
  4.2 78.6 %experts.1 = bf16[6,512]{1,0:T(8,128)(2,1)} custom-call(bf16[2,8,384]{2,1,0:T(8,128)(2,1)} %pad_maximum_fusion.msg_ref, f32[8,128]{1,0:T(8,128)} %pad.13.comb_ref, bf16[4096,128]{1,0:T(8,128)(2,1)} %bitcast.7, bf16[4096,128]{1,0:T(8,128)(2,1)} %bitcast.8, bf16[64,8192]{1,0:T(8,128)(2,1)} %bitcast.9), custom_call_target="tpu_custom_call" | custom-call | tf_op jit(solution)/shard_map/experts/pallas_call | solution.py:358
  82.9 1.3 %copy.14 = bf16[6,512]{1,0:T(8,128)(2,1)} copy(bf16[6,512]{1,0:T(8,128)(2,1)} %experts.1) | data formatting | bytes 12288
  (11 shorter events, 0.1 us)
Async XLA Ops:
  1.1 0.7 copy-start
  2.5 0.7 copy-start.1

commit v2 on v1

v2 whole, which is shorter than its diff:
```python
import functools

import jax
import jax.numpy as jnp
from jax import lax
from jax.experimental import pallas as pl
from jax.experimental.pallas import tpu as pltpu
from jax.sharding import Mesh
from jax.sharding import PartitionSpec as P

SHARD = ("shard_0", "shard_1")
MESH = pl.DeviceIdType.MESH
NARROW = ("shard_1", "shard_0")
WIDE = ("shard_0", "shard_1")
CHUNKS = 2
SPAN = 64
F32, BF16 = jnp.float32, jnp.bfloat16


def kernel(
    n, cap, tok_hbm, ids_hbm, gates_hbm, gate_hbm, up_hbm, down_hbm, out_ref,
    tok_v, ids_v, gates_v, stage, toks, sel, rows, part, hid, acc, give, got, got32, pass_on, back,
    gate_w, up_w, down_w,
    load_sem, a1_send, a1_recv, a2_send, a2_recv, a3_send, a3_recv,
    c1_send, c1_recv, c2_send, c2_recv, e1_send, e1_recv, e2_send, e2_recv,
):
    e = lax.axis_index("expert")
    y = lax.axis_index("shard_0")
    z = lax.axis_index("shard_1")
    nar = (z, y)
    wid = (y, z)
    top = n // 2
    cells = n * n
    hcells = cells // 2
    tok_count, feats = tok_v.shape
    half = feats // 2
    hidden_units = gate_w.shape[1]
    per = n // CHUNKS
    far = [d for k in range(top) for d in sorted({top - k, top + k}) if d < n]

    def plus(a, b):
        return lax.rem(a + b + n, n)

    small = [
        pltpu.make_async_copy(ids_hbm, ids_v, load_sem.at[0]),
        pltpu.make_async_copy(gates_hbm, gates_v, load_sem.at[1]),
        pltpu.make_async_copy(tok_hbm, tok_v, load_sem.at[2]),
    ]
    loads = [
        pltpu.make_async_copy(gate_hbm, gate_w, load_sem.at[3]),
        pltpu.make_async_copy(up_hbm, up_w, load_sem.at[4]),
        pltpu.make_async_copy(down_hbm, down_w.at[0], load_sem.at[5]),
        pltpu.make_async_copy(down_hbm, down_w.at[1], load_sem.at[6]),
    ]
    for copy in small:
        copy.start()
    barrier = pltpu.get_barrier_semaphore()
    for d in far:
        for axis, own in (("shard_1", z), ("shard_0", y), ("expert", e)):
            pl.semaphore_signal(
                barrier, inc=1, device_id={axis: plus(own, d)}, device_id_type=MESH
            )
    for copy in small:
        copy.wait()
    for copy in loads:
        copy.start()

    ids = [[ids_v[k : k + 1, t : t + 1] for t in range(tok_count)] for k in range(2)]
    amount = [[gates_v[k : k + 1, t : t + 1] for t in range(tok_count)] for k in range(2)]

    def codes_of(expert):
        run = jnp.zeros(expert.shape, F32)
        out = []
        for t in range(tok_count):
            hit = (ids[0][t] == expert) | (ids[1][t] == expert)
            out.append(jnp.where(hit, run + 1.0, 0.0))
            run = run + jnp.where(hit, 1.0, 0.0)
        return out

    sub = lax.broadcasted_iota(jnp.int32, (8, half), 0)
    lane = lax.broadcasted_iota(jnp.int32, (8, half), 1)
    held = half // SPAN
    expert = jnp.where(sub >= 6, (sub - 6) * held + lane // SPAN, -1)
    codes = codes_of(expert)
    stage[...] = jnp.zeros_like(stage)
    stage[0:tok_count, :] = tok_v[...].astype(F32)
    for h in range(2):
        here = (lane % SPAN) // 8 == nar[h]
        spare = jnp.zeros((8, half), F32)
        for t in range(tok_count):
            spare = jnp.where(here & (lane % 8 == t), codes[t], spare)
        toks[h, nar[h]] = (stage[:, h * half : (h + 1) * half] + spare).astype(BF16)

    pl.semaphore_wait(barrier, 3 * (n - 1))

    def a1(h, d):
        block = toks.at[h, nar[h]]
        return pltpu.make_async_remote_copy(
            src_ref=block,
            dst_ref=block,
            send_sem=a1_send.at[h, d],
            recv_sem=a1_recv.at[h, d],
            device_id={NARROW[h]: plus(nar[h], -d)},
            device_id_type=MESH,
        )

    for d in far:
        for h in range(2):
            a1(h, d).start()

    def a2(h, d):
        return pltpu.make_async_remote_copy(
            src_ref=sel.at[h, plus(e, -d)],
            dst_ref=rows.at[h, :, wid[h], d],
            send_sem=a2_send.at[h, d],
            recv_sem=a2_recv.at[h, d],
            device_id={"expert": plus(e, -d)},
            device_id_type=MESH,
        )

    m = held * cap * n
    row_of = lax.broadcasted_iota(jnp.int32, (m, half), 0)
    lane_of = lax.broadcasted_iota(jnp.int32, (m, half), 1)
    meets = ((lane_of % SPAN) // 8 == row_of % n) & (lane_of // SPAN == row_of // (cap * n))
    wanted = jnp.where(meets, ((row_of // n) % cap + 1).astype(F32), -1.0)
    for h in range(2):
        for d in far:
            a1(h, d).wait_recv()
        marks = jnp.zeros((8, half), F32)
        for b in range(n):
            marks = marks + toks[h, b].astype(F32)
        block = toks[h].reshape(8 * n, half)
        if 8 * n < SPAN:
            block = jnp.concatenate([block, jnp.zeros((SPAN - 8 * n, half), BF16)], axis=0)
        block = jnp.concatenate([block] * held, axis=0)
        pick = jnp.concatenate(
            [jnp.where(marks[6 + r : 7 + r, :] == wanted, 1.0, 0.0) for r in range(n // held)],
            axis=0,
        ).astype(BF16)
        found = jnp.dot(pick, block, preferred_element_type=F32)
        sel[h] = found.reshape(n, cap, n, half).astype(BF16)
        for d in range(1, n):
            a2(h, d).start()
        rows[h, :, wid[h], 0] = sel[h, e]

    def a3(h, s, way, k, j):
        step = 1 if way == 0 else -1
        unit = rows.at[h, s, plus(wid[h], -step * (k - 1)), pl.ds(j * per, per)]
        return pltpu.make_async_remote_copy(
            src_ref=unit,
            dst_ref=unit,
            send_sem=a3_send.at[h, s, way, k - 1, j],
            recv_sem=a3_recv.at[h, s, way, k - 1, j],
            device_id={WIDE[h]: plus(wid[h], step)},
            device_id_type=MESH,
        )

    def split(way, k, j, count):
        return k < top or (j < count // 2) == (way == 0)

    for j in range(CHUNKS):
        for h in range(2):
            for d in range(j * per, (j + 1) * per):
                if d > 0:
                    a2(h, d).wait_recv()
        for s in range(cap):
            for h in range(2):
                for way in range(2):
                    if split(way, 1, j, CHUNKS):
                        a3(h, s, way, 1, j).start()

    order = [0]
    for d in range(1, top):
        order += [d, n - d]
    order.append(top)
    place = {d: p for p, d in enumerate(order)}

    def c1(h, s, way, k):
        step = -1 if way == 0 else 1
        return pltpu.make_async_remote_copy(
            src_ref=hid.at[h, s, wid[h], place[(-step * (k - 1)) % n]],
            dst_ref=hid.at[h, s, wid[h], place[(-step * k) % n]],
            send_sem=c1_send.at[h, s, way, k - 1],
            recv_sem=c1_recv.at[h, s, way, k - 1],
            device_id={NARROW[h]: plus(nar[h], step)},
            device_id_type=MESH,
        )

    def in_line(s, way, k):
        return k < top or way == s % 2

    def c2(h, s, way, k, i):
        step = 1 if way == 0 else -1
        unit = hid.at[h, s, plus(wid[h], -step * (k - 1)), pl.ds(2 * i, 2)]
        return pltpu.make_async_remote_copy(
            src_ref=unit,
            dst_ref=unit,
            send_sem=c2_send.at[h, s, way, k - 1, i],
            recv_sem=c2_recv.at[h, s, way, k - 1, i],
            device_id={WIDE[h]: plus(wid[h], step)},
            device_id_type=MESH,
        )

    def project(s):
        sums = []
        for h in range(2):
            total = jnp.zeros((cells, 2 * hidden_units), F32)
            for d in range(n):
                at = pl.multiple_of(plus(e, d) * (2 * half) + h * half, half)
                lhs = rows[h, s, :, d].reshape(cells, half)
                rhs = jnp.concatenate(
                    [gate_w[pl.ds(at, half), :], up_w[pl.ds(at, half), :]], axis=1
                )
                total = total + jnp.dot(lhs, rhs, preferred_element_type=F32)
            sums.append(total)
        for c in range(2):
            part[c] = sums[0][:, c * hidden_units : (c + 1) * hidden_units]
        gated, up = (
            jnp.concatenate([part[c, pl.ds(b, n, stride=n), :] for b in range(n)], axis=0)
            + sums[1][:, c * hidden_units : (c + 1) * hidden_units]
            for c in range(2)
        )
        hidden = ((gated / (1.0 + jnp.exp(-gated))) * up).astype(BF16)
        for h in range(2):
            hid[h, s, wid[h], 0] = hidden[h * hcells : (h + 1) * hcells, :]

    for k in range(1, top + 1):
        if k == top:
            for copy in loads:
                copy.wait()
        for s in range(cap):
            for j in range(CHUNKS):
                for h in range(2):
                    for way in range(2):
                        if split(way, k, j, CHUNKS):
                            a3(h, s, way, k, j).wait_recv()
                        if k < top and split(way, k + 1, j, CHUNKS):
                            a3(h, s, way, k + 1, j).start()
            if k == top:
                project(s)
                for h in range(2):
                    for way in range(2):
                        if in_line(s, way, 1):
                            c1(h, s, way, 1).start()

    acc[...] = jnp.zeros_like(acc)
    pairs = n // 2

    def use(h, src, i):
        lhs, rhs = [], []
        for p in (2 * i, 2 * i + 1):
            other = plus(nar[h], order[p])
            unit = src * n + other if h == 0 else other * n + src
            at = pl.multiple_of(unit * hidden_units, hidden_units)
            lhs.append(hid[h, :, src, p].reshape(cap * hcells, hidden_units))
            rhs.append(down_w[:, :, pl.ds(at, hidden_units)].reshape(128, hidden_units))
        acc[h] += lax.dot_general(
            jnp.concatenate(lhs, axis=1),
            jnp.concatenate(rhs, axis=1),
            (((1,), (1,)), ((), ())),
            preferred_element_type=F32,
        )

    def use_slot(slot):
        for h in range(2):
            if 1 <= slot <= pairs:
                use(h, wid[h], slot - 1)
            for i in range(pairs):
                k = slot - 1 - i
                if 1 <= k < top:
                    use(h, plus(wid[h], -k), i)
                    use(h, plus(wid[h], k), i)
                elif k == top:
                    use(h, plus(wid[h], k), i)

    last = pairs + top
    for slot in range(1, last + 1):
        if slot == last:
            use_slot(slot - 1)
        for s in range(cap):
            for h in range(2):
                if slot <= top:
                    for way in range(2):
                        if in_line(s, way, slot):
                            c1(h, s, way, slot).wait_recv()
                        if slot < top and in_line(s, way, slot + 1):
                            c1(h, s, way, slot + 1).start()
                if slot <= pairs:
                    for way in range(2):
                        if split(way, 1, slot - 1, pairs):
                            c2(h, s, way, 1, slot - 1).start()
                for i in range(pairs):
                    k = slot - 1 - i
                    if 1 <= k <= top:
                        for way in range(2):
                            if split(way, k, i, pairs):
                                c2(h, s, way, k, i).wait_recv()
                            if k < top and split(way, k + 1, i, pairs):
                                c2(h, s, way, k + 1, i).start()
        if slot < last:
            use_slot(slot - 1)
    use_slot(last)

    def e1(d):
        return pltpu.make_async_remote_copy(
            src_ref=give.at[plus(z, -d)],
            dst_ref=got.at[z],
            send_sem=e1_send.at[d],
            recv_sem=e1_recv.at[d],
            device_id={"shard_1": plus(z, -d)},
            device_id_type=MESH,
        )

    for a in range(n):
        for s in range(cap):
            at = s * hcells + (a % top) * n
            give[a, s] = acc[a // top, at : at + n, :].astype(BF16)
    for d in far:
        e1(d).start()
    got[z] = give[z]

    at_tok = lax.broadcasted_iota(jnp.int32, (8, 128), 0)
    at_row = lax.broadcasted_iota(jnp.int32, (8, 128), 1)
    whose = jnp.where(at_row < n * cap, at_row // cap, -1)
    coefs = jnp.zeros((8, 128), F32)
    for t, code in enumerate(codes_of(whose)):
        weight = jnp.where(ids[0][t] == whose, amount[0][t], 0.0) + jnp.where(
            ids[1][t] == whose, amount[1][t], 0.0
        )
        mine = (at_tok == t) & (code == (at_row % cap + 1).astype(F32))
        coefs = jnp.where(mine, weight, coefs)

    for d in far:
        e1(d).wait_recv()
    got32[...] = got[...].astype(F32).reshape(got32.shape)
    for b in range(n):
        mine = got32[pl.ds(b, n * cap, stride=n), :]
        pass_on[b] = mine.reshape(cap, n, 128).astype(BF16)

    def e2(b, src):
        return pltpu.make_async_remote_copy(
            src_ref=pass_on.at[b],
            dst_ref=back.at[src],
            send_sem=e2_send.at[b],
            recv_sem=e2_recv.at[src],
            device_id={"expert": y, "shard_0": b},
            device_id_type=MESH,
        )

    for b in range(n):
        here = (e == y) & (y == b)

        @pl.when(jnp.logical_not(here))
        def _(b=b):
            e2(b, e).start()

        @pl.when(here)
        def _(b=b):
            back[e] = pass_on[b]

    for src in range(n):

        @pl.when(jnp.logical_not((src == e) & (y == e)))
        def _(src=src):
            e2(0, src).wait_recv()

    low = lax.broadcasted_iota(jnp.int32, (1, 128), 1) < 64
    sums = [jnp.zeros((8, 128), F32) for _ in range(n // 2)]
    for src in range(n):
        value = back[src].astype(F32).reshape(n * cap, 128)
        for s in range(cap):
            at = src * cap + s
            coef = coefs[:, at : at + 1]
            for g in range(n // 2):
                a, b = 2 * g * cap + s, (2 * g + 1) * cap + s
                sums[g] = sums[g] + coef * jnp.where(low, value[a : a + 1, :], value[b : b + 1, :])
    for g in range(n // 2):
        out_ref[:, g * 128 : (g + 1) * 128] = sums[g][:tok_count, :].astype(BF16)

    for h in range(2):
        for d in range(1, n):
            a1(h, d).wait_send()
            a2(h, d).wait_send()
        for s in range(cap):
            for way in range(2):
                for k in range(1, top + 1):
                    for j in range(CHUNKS):
                        if split(way, k, j, CHUNKS):
                            a3(h, s, way, k, j).wait_send()
                    if in_line(s, way, k):
                        c1(h, s, way, k).wait_send()
                    for i in range(pairs):
                        if split(way, k, i, pairs):
                            c2(h, s, way, k, i).wait_send()
    for d in range(1, n):
        e1(d).wait_send()
    for b in range(n):

        @pl.when(jnp.logical_not((e == y) & (y == b)))
        def _(b=b):
            e2(b, e).wait_send()


def shards(n, tokens, expert_ids, gates, gate_proj, up_proj, down_proj_t):
    tok_count, feats = tokens.shape
    half = feats // 2
    hidden_units = gate_proj.shape[2]
    out_feats = down_proj_t.shape[1]
    cap = min(tok_count, 4 * tok_count // n)
    cells = n * n
    top = n // 2
    dma = pltpu.SemaphoreType.DMA
    vmem = pltpu.VMEM
    return pl.pallas_call(
        functools.partial(kernel, n, cap),
        out_shape=jax.ShapeDtypeStruct((tok_count, feats), BF16),
        in_specs=[pl.BlockSpec(memory_space=pl.ANY)] * 6,
        out_specs=pl.BlockSpec(memory_space=vmem),
        scratch_shapes=[
            vmem(tokens.shape, BF16),
            vmem((2, tok_count), jnp.int32),
            vmem((2, tok_count), F32),
            vmem((8, feats), F32),
            vmem((2, n, 8, half), BF16),
            vmem((2, n, cap, n, half), BF16),
            vmem((2, cap, n, n, n, half), BF16),
            vmem((2, cells, hidden_units), F32),
            vmem((2, cap, n, n, cells // 2, hidden_units), BF16),
            vmem((2, cap * cells // 2, 128), F32),
            vmem((n, cap, n, 128), BF16),
            vmem((n, cap, n, 128), BF16),
            vmem((n * cap * n, 128), F32),
            vmem((n, cap, n, 128), BF16),
            vmem((n, cap, n, 128), BF16),
            vmem(gate_proj.shape[1:], BF16),
            vmem(up_proj.shape[1:], BF16),
            vmem((2, out_feats, down_proj_t.shape[2]), BF16),
            dma((7,)),
            dma((2, n)), dma((2, n)),
            dma((2, n)), dma((2, n)),
            dma((2, cap, 2, top, CHUNKS)), dma((2, cap, 2, top, CHUNKS)),
            dma((2, cap, 2, top)), dma((2, cap, 2, top)),
            dma((2, cap, 2, top, n // 2)), dma((2, cap, 2, top, n // 2)),
            dma((n,)), dma((n,)),
            dma((n,)), dma((n,)),
        ],
        compiler_params=pltpu.CompilerParams(collective_id=0, has_side_effects=True),
        name="experts",
    )(tokens, expert_ids.T, gates.T, gate_proj[0], up_proj[0], down_proj_t[0])


def solution(mesh):
    n = mesh.shape["expert"]
    split = Mesh(mesh.devices.reshape(n, n, n), ("expert", "shard_0", "shard_1"))
    placed = (
        P(SHARD, "expert"),
        P(SHARD, None),
        P(SHARD, None),
        P("expert", None, SHARD),
        P("expert", None, SHARD),
        P("expert", SHARD, None),
    )
    return jax.shard_map(
        functools.partial(shards, n),
        mesh=split,
        in_specs=placed,
        out_specs=P(SHARD, "expert"),
        check_vma=False,
    )
```

time: 85 us -> 85.1 us (level)
  Pallas kernels: 78.6 us -> 83.6 us
  local copies, waits for them, and re-layouts: 4.43 us -> 1.3 us
  other arithmetic: 1.08 us -> 0 us
    pallas_call x1, Pallas kernels: 78.6 us -> 83.6 us  [shards(): pl.pallas_call(functools.partial(kernel, n, cap), out_shape=jax.ShapeDtyp...]
    unnamed x7 -> x1, local copies, waits for them, and re-layouts: 3.44 us -> 1.3 us
where the time goes in v2:
time: 85.1 us; the launch traced here: 84.9 us
  Pallas kernels  83.6 us (98%)
  local copies, waits for them, and re-layouts  1.3 us (2%)
    pallas_call x1, Pallas kernels, shards(): pl.pallas_call(functools.partial(kernel, n, cap), out_shape=jax.ShapeDtyp...  83.6 us

profile of v2, /device:TPU:1, one launch (start us, length us, event | category | flops | bytes accessed | tf_op | source)
XLA Modules:
  0.0 84.9 jit_solution(11688485245123473970)
XLA Ops:
  0.0 83.6 %experts.1 = bf16[6,512]{1,0:T(8,128)(2,1)} custom-call(bf16[6,512]{1,0:T(8,128)(2,1)} %tok_hbm.1, s32[2,6]{1,0:T(2,128)} %bitcast.8, f32[2,6]{1,0:T(2,128)} %bitcast.9, bf16[4096,128]{1,0:T(8,128)(2,1)} %bitcast.5, bf16[4096,128]{1,0:T(8,128)(2,1)} %bitcast.6, bf16[64,8192]{1,0:T(8,128)(2,1)} %bitcast.7), custom_call_target="tpu_custom_call" | custom-call | tf_op jit(solution)/shard_map/experts/pallas_call | solution.py:414
  83.6 1.3 %copy.8 = bf16[6,512]{1,0:T(8,128)(2,1)} copy(bf16[6,512]{1,0:T(8,128)(2,1)} %experts.1) | data formatting | bytes 12288

commit v3 on v2

--- a/solution.py
+++ b/solution.py
@@ -13,6 +13,7 @@
 NARROW = ("shard_1", "shard_0")
 WIDE = ("shard_0", "shard_1")
 CHUNKS = 2
+LEAPS = (0, 1, 2)
 SPAN = 64
 F32, BF16 = jnp.float32, jnp.bfloat16
 
@@ -145,13 +146,14 @@
 
     def a3(h, s, way, k, j):
         step = 1 if way == 0 else -1
-        unit = rows.at[h, s, plus(wid[h], -step * (k - 1)), pl.ds(j * per, per)]
+        base = k - 1 if s not in LEAPS else (0 if k <= 2 else 2)
+        unit = rows.at[h, s, plus(wid[h], -step * base), pl.ds(j * per, per)]
         return pltpu.make_async_remote_copy(
             src_ref=unit,
             dst_ref=unit,
             send_sem=a3_send.at[h, s, way, k - 1, j],
             recv_sem=a3_recv.at[h, s, way, k - 1, j],
-            device_id={WIDE[h]: plus(wid[h], step)},
+            device_id={WIDE[h]: plus(wid[h], step * (k - base))},
             device_id_type=MESH,
         )
 
@@ -166,8 +168,20 @@
         for s in range(cap):
             for h in range(2):
                 for way in range(2):
-                    if split(way, 1, j, CHUNKS):
-                        a3(h, s, way, 1, j).start()
+                    for k in (2, 1) if s in LEAPS else (1,):
+                        if k <= top and split(way, k, j, CHUNKS):
+                            a3(h, s, way, k, j).start()
+
+    def pass_rows(s, k):
+        for j in range(CHUNKS):
+            for h in range(2):
+                for way in range(2):
+                    if split(way, k, j, CHUNKS):
+                        a3(h, s, way, k, j).wait_recv()
+                    after = (k + 1,) if s not in LEAPS else ((4, 3) if k == 2 else ())
+                    for later in after:
+                        if later <= top and split(way, later, j, CHUNKS):
+                            a3(h, s, way, later, j).start()
 
     order = [0]
     for d in range(1, top):
@@ -175,19 +189,16 @@
     order.append(top)
     place = {d: p for p, d in enumerate(order)}
 
-    def c1(h, s, way, k):
-        step = -1 if way == 0 else 1
-        return pltpu.make_async_remote_copy(
-            src_ref=hid.at[h, s, wid[h], place[(-step * (k - 1)) % n]],
-            dst_ref=hid.at[h, s, wid[h], place[(-step * k) % n]],
-            send_sem=c1_send.at[h, s, way, k - 1],
-            recv_sem=c1_recv.at[h, s, way, k - 1],
-            device_id={NARROW[h]: plus(nar[h], step)},
-            device_id_type=MESH,
-        )
-
-    def in_line(s, way, k):
-        return k < top or way == s % 2
+    def c1(h, s, d):
+        send, to = (0, -d) if d != top else ((top - 1, -1) if s % 2 == 0 else ((1 - top) % n, 1))
+        return pltpu.make_async_remote_copy(
+            src_ref=hid.at[h, s, wid[h], place[send]],
+            dst_ref=hid.at[h, s, wid[h], place[d]],
+            send_sem=c1_send.at[h, s, d],
+            recv_sem=c1_recv.at[h, s, d],
+            device_id={NARROW[h]: plus(nar[h], to)},
+            device_id_type=MESH,
+        )
 
     def c2(h, s, way, k, i):
         step = 1 if way == 0 else -1
@@ -224,24 +235,35 @@
         for h in range(2):
             hid[h, s, wid[h], 0] = hidden[h * hcells : (h + 1) * hcells, :]
 
+    def begin(s):
+        project(s)
+        for k in range(top - 1, 0, -1):
+            for d in (k, n - k):
+                for h in range(2):
+                    c1(h, s, d).start()
+        if top == 1:
+            for h in range(2):
+                c1(h, s, top).start()
+
+    slow = [s for s in range(cap) if s not in LEAPS]
+    quick = [s for s in range(cap) if s in LEAPS]
     for k in range(1, top + 1):
-        if k == top:
+        for s in slow if k < top else ():
+            pass_rows(s, k)
+        if k == 2 or k == top == 1:
+            for s in quick:
+                for q in range(1, min(top, 2) + 1):
+                    pass_rows(s, q)
+        if k == min(3, top):
             for copy in loads:
                 copy.wait()
-        for s in range(cap):
-            for j in range(CHUNKS):
-                for h in range(2):
-                    for way in range(2):
-                        if split(way, k, j, CHUNKS):
-                            a3(h, s, way, k, j).wait_recv()
-                        if k < top and split(way, k + 1, j, CHUNKS):
-                            a3(h, s, way, k + 1, j).start()
-            if k == top:
-                project(s)
-                for h in range(2):
-                    for way in range(2):
-                        if in_line(s, way, 1):
-                            c1(h, s, way, 1).start()
+            for s in quick:
+                for q in range(3, top + 1):
+                    pass_rows(s, q)
+                begin(s)
+    for s in slow:
+        pass_rows(s, top)
+        begin(s)
 
     acc[...] = jnp.zeros_like(acc)
     pairs = n // 2
@@ -261,45 +283,55 @@
             preferred_element_type=F32,
         )
 
-    def use_slot(slot):
+    early = pairs - 1
+
+    def use_step(t):
         for h in range(2):
-            if 1 <= slot <= pairs:
-                use(h, wid[h], slot - 1)
             for i in range(pairs):
-                k = slot - 1 - i
-                if 1 <= k < top:
+                k = t if i < early else t - 1
+                if k == 0:
+                    use(h, wid[h], i)
+                elif 1 <= k < top:
                     use(h, plus(wid[h], -k), i)
                     use(h, plus(wid[h], k), i)
                 elif k == top:
                     use(h, plus(wid[h], k), i)
 
-    last = pairs + top
-    for slot in range(1, last + 1):
-        if slot == last:
-            use_slot(slot - 1)
+    def launch(h, s, i):
+        for way in range(2):
+            if split(way, 1, i, pairs):
+                c2(h, s, way, 1, i).start()
+
+    def pass_hidden(h, s, k, i):
+        for way in range(2):
+            if split(way, k, i, pairs):
+                c2(h, s, way, k, i).wait_recv()
+            if k < top and split(way, k + 1, i, pairs):
+                c2(h, s, way, k + 1, i).start()
+
+    for s in range(cap):
+        for h in range(2):
+            for p in range(1, n - 1):
+                c1(h, s, order[p]).wait_recv()
+                if p % 2 == 1:
+                    launch(h, s, p // 2)
+                if top > 1 and order[p] == (top - 1 if s % 2 == 0 else n - top + 1):
+                    c1(h, s, top).start()
+    for t in range(1, top + 2):
+        if t == top + 1:
+            use_step(top)
         for s in range(cap):
             for h in range(2):
-                if slot <= top:
-                    for way in range(2):
-                        if in_line(s, way, slot):
-                            c1(h, s, way, slot).wait_recv()
-                        if slot < top and in_line(s, way, slot + 1):
-                            c1(h, s, way, slot + 1).start()
-                if slot <= pairs:
-                    for way in range(2):
-                        if split(way, 1, slot - 1, pairs):
-                            c2(h, s, way, 1, slot - 1).start()
-                for i in range(pairs):
-                    k = slot - 1 - i
-                    if 1 <= k <= top:
-                        for way in range(2):
-                            if split(way, k, i, pairs):
-                                c2(h, s, way, k, i).wait_recv()
-                            if k < top and split(way, k + 1, i, pairs):
-                                c2(h, s, way, k + 1, i).start()
-        if slot < last:
-            use_slot(slot - 1)
-    use_slot(last)
+                for i in range(early if t <= top else 0):
+                    pass_hidden(h, s, t, i)
+                if t == 1:
+                    c1(h, s, top).wait_recv()
+                    launch(h, s, pairs - 1)
+                else:
+                    pass_hidden(h, s, t - 1, pairs - 1)
+        if t <= top:
+            use_step(t - 1)
+    use_step(top + 1)
 
     def e1(d):
         return pltpu.make_async_remote_copy(
@@ -382,13 +414,13 @@
             a1(h, d).wait_send()
             a2(h, d).wait_send()
         for s in range(cap):
+            for d in range(1, n):
+                c1(h, s, d).wait_send()
             for way in range(2):
                 for k in range(1, top + 1):
                     for j in range(CHUNKS):
                         if split(way, k, j, CHUNKS):
                             a3(h, s, way, k, j).wait_send()
-                    if in_line(s, way, k):
-                        c1(h, s, way, k).wait_send()
                     for i in range(pairs):
                         if split(way, k, i, pairs):
                             c2(h, s, way, k, i).wait_send()
@@ -439,7 +471,7 @@
             dma((2, n)), dma((2, n)),
             dma((2, n)), dma((2, n)),
             dma((2, cap, 2, top, CHUNKS)), dma((2, cap, 2, top, CHUNKS)),
-            dma((2, cap, 2, top)), dma((2, cap, 2, top)),
+            dma((2, cap, n)), dma((2, cap, n)),
             dma((2, cap, 2, top, n // 2)), dma((2, cap, 2, top, n // 2)),
             dma((n,)), dma((n,)),
             dma((n,)), dma((n,)),

time: 85.1 us -> 78.9 us (0.927)
  Pallas kernels: 83.6 us -> 77.3 us
    pallas_call x1, Pallas kernels: 83.6 us -> 77.3 us  [shards(): pl.pallas_call(functools.partial(kernel, n, cap), out_shape=jax.ShapeDtyp...]
where the time goes in v3:
time: 78.9 us; the launch traced here: 78.6 us
  Pallas kernels  77.3 us (98%)
  local copies, waits for them, and re-layouts  1.3 us (2%)
    pallas_call x1, Pallas kernels, shards(): pl.pallas_call(functools.partial(kernel, n, cap), out_shape=jax.ShapeDtyp...  77.3 us

profile of v3, /device:TPU:1, one launch (start us, length us, event | category | flops | bytes accessed | tf_op | source)
XLA Modules:
  0.0 78.6 jit_solution(1670533599983781449)
XLA Ops:
  0.0 77.3 %experts.1 = bf16[6,512]{1,0:T(8,128)(2,1)} custom-call(bf16[6,512]{1,0:T(8,128)(2,1)} %tok_hbm.1, s32[2,6]{1,0:T(2,128)} %bitcast.8, f32[2,6]{1,0:T(2,128)} %bitcast.9, bf16[4096,128]{1,0:T(8,128)(2,1)} %bitcast.5, bf16[4096,128]{1,0:T(8,128)(2,1)} %bitcast.6, bf16[64,8192]{1,0:T(8,128)(2,1)} %bitcast.7), custom_call_target="tpu_custom_call" | custom-call | tf_op jit(solution)/shard_map/experts/pallas_call | solution.py:446
  77.3 1.3 %copy.8 = bf16[6,512]{1,0:T(8,128)(2,1)} copy(bf16[6,512]{1,0:T(8,128)(2,1)} %experts.1) | data formatting | bytes 12288

commit v4 on v3

--- a/solution.py
+++ b/solution.py
@@ -94,13 +94,16 @@
 
     pl.semaphore_wait(barrier, 3 * (n - 1))
 
+    def bytes_of(ref, sem):
+        return pltpu.make_async_copy(ref, ref, sem).wait()
+
     def a1(h, d):
         block = toks.at[h, nar[h]]
         return pltpu.make_async_remote_copy(
             src_ref=block,
             dst_ref=block,
-            send_sem=a1_send.at[h, d],
-            recv_sem=a1_recv.at[h, d],
+            send_sem=a1_send.at[h],
+            recv_sem=a1_recv.at[h],
             device_id={NARROW[h]: plus(nar[h], -d)},
             device_id_type=MESH,
         )
@@ -113,8 +116,8 @@
         return pltpu.make_async_remote_copy(
             src_ref=sel.at[h, plus(e, -d)],
             dst_ref=rows.at[h, :, wid[h], d],
-            send_sem=a2_send.at[h, d],
-            recv_sem=a2_recv.at[h, d],
+            send_sem=a2_send.at[h],
+            recv_sem=a2_recv.at[h, d // per],
             device_id={"expert": plus(e, -d)},
             device_id_type=MESH,
         )
@@ -125,8 +128,7 @@
     meets = ((lane_of % SPAN) // 8 == row_of % n) & (lane_of // SPAN == row_of // (cap * n))
     wanted = jnp.where(meets, ((row_of // n) % cap + 1).astype(F32), -1.0)
     for h in range(2):
-        for d in far:
-            a1(h, d).wait_recv()
+        bytes_of(toks.at[h, pl.ds(0, n - 1)], a1_recv.at[h])
         marks = jnp.zeros((8, half), F32)
         for b in range(n):
             marks = marks + toks[h, b].astype(F32)
@@ -151,7 +153,7 @@
         return pltpu.make_async_remote_copy(
             src_ref=unit,
             dst_ref=unit,
-            send_sem=a3_send.at[h, s, way, k - 1, j],
+            send_sem=a3_send.at[h, s],
             recv_sem=a3_recv.at[h, s, way, k - 1, j],
             device_id={WIDE[h]: plus(wid[h], step * (k - base))},
             device_id_type=MESH,
@@ -162,9 +164,9 @@
 
     for j in range(CHUNKS):
         for h in range(2):
-            for d in range(j * per, (j + 1) * per):
-                if d > 0:
-                    a2(h, d).wait_recv()
+            count = per if j > 0 else per - 1
+            if count > 0:
+                bytes_of(sel.at[h, pl.ds(0, count)], a2_recv.at[h, j])
         for s in range(cap):
             for h in range(2):
                 for way in range(2):
@@ -194,7 +196,7 @@
         return pltpu.make_async_remote_copy(
             src_ref=hid.at[h, s, wid[h], place[send]],
             dst_ref=hid.at[h, s, wid[h], place[d]],
-            send_sem=c1_send.at[h, s, d],
+            send_sem=c1_send.at[h, s],
             recv_sem=c1_recv.at[h, s, d],
             device_id={NARROW[h]: plus(nar[h], to)},
             device_id_type=MESH,
@@ -206,7 +208,7 @@
         return pltpu.make_async_remote_copy(
             src_ref=unit,
             dst_ref=unit,
-            send_sem=c2_send.at[h, s, way, k - 1, i],
+            send_sem=c2_send.at[h, s],
             recv_sem=c2_recv.at[h, s, way, k - 1, i],
             device_id={WIDE[h]: plus(wid[h], step)},
             device_id_type=MESH,
@@ -337,8 +339,8 @@
         return pltpu.make_async_remote_copy(
             src_ref=give.at[plus(z, -d)],
             dst_ref=got.at[z],
-            send_sem=e1_send.at[d],
-            recv_sem=e1_recv.at[d],
+            send_sem=e1_send,
+            recv_sem=e1_recv,
             device_id={"shard_1": plus(z, -d)},
             device_id_type=MESH,
         )
@@ -362,8 +364,14 @@
         mine = (at_tok == t) & (code == (at_row % cap + 1).astype(F32))
         coefs = jnp.where(mine, weight, coefs)
 
-    for d in far:
-        e1(d).wait_recv()
+    for h in range(2):
+        bytes_of(toks.at[h, pl.ds(0, n - 1)], a1_send.at[h])
+        bytes_of(sel.at[h, pl.ds(0, n - 1)], a2_send.at[h])
+        for s in range(cap):
+            bytes_of(rows.at[h, s, pl.ds(0, n - 1)], a3_send.at[h, s])
+            bytes_of(hid.at[h, s, 0, pl.ds(0, n - 1)], c1_send.at[h, s])
+            bytes_of(hid.at[h, s, pl.ds(0, n - 1)], c2_send.at[h, s])
+    bytes_of(give.at[pl.ds(0, n - 1)], e1_recv)
     got32[...] = got[...].astype(F32).reshape(got32.shape)
     for b in range(n):
         mine = got32[pl.ds(b, n * cap, stride=n), :]
@@ -373,8 +381,8 @@
         return pltpu.make_async_remote_copy(
             src_ref=pass_on.at[b],
             dst_ref=back.at[src],
-            send_sem=e2_send.at[b],
-            recv_sem=e2_recv.at[src],
+            send_sem=e2_send,
+            recv_sem=e2_recv,
             device_id={"expert": y, "shard_0": b},
             device_id_type=MESH,
         )
@@ -390,11 +398,13 @@
         def _(b=b):
             back[e] = pass_on[b]
 
-    for src in range(n):
-
-        @pl.when(jnp.logical_not((src == e) & (y == e)))
-        def _(src=src):
-            e2(0, src).wait_recv()
+    @pl.when(e == y)
+    def _():
+        bytes_of(back.at[pl.ds(0, n - 1)], e2_recv)
+
+    @pl.when(e != y)
+    def _():
+        bytes_of(back, e2_recv)
 
     low = lax.broadcasted_iota(jnp.int32, (1, 128), 1) < 64
     sums = [jnp.zeros((8, 128), F32) for _ in range(n // 2)]
@@ -409,28 +419,15 @@
     for g in range(n // 2):
         out_ref[:, g * 128 : (g + 1) * 128] = sums[g][:tok_count, :].astype(BF16)
 
-    for h in range(2):
-        for d in range(1, n):
-            a1(h, d).wait_send()
-            a2(h, d).wait_send()
-        for s in range(cap):
-            for d in range(1, n):
-                c1(h, s, d).wait_send()
-            for way in range(2):
-                for k in range(1, top + 1):
-                    for j in range(CHUNKS):
-                        if split(way, k, j, CHUNKS):
-                            a3(h, s, way, k, j).wait_send()
-                    for i in range(pairs):
-                        if split(way, k, i, pairs):
-                            c2(h, s, way, k, i).wait_send()
-    for d in range(1, n):
-        e1(d).wait_send()
-    for b in range(n):
-
-        @pl.when(jnp.logical_not((e == y) & (y == b)))
-        def _(b=b):
-            e2(b, e).wait_send()
+    bytes_of(give.at[pl.ds(0, n - 1)], e1_send)
+
+    @pl.when(e == y)
+    def _():
+        bytes_of(pass_on.at[pl.ds(0, n - 1)], e2_send)
+
+    @pl.when(e != y)
+    def _():
+        bytes_of(pass_on, e2_send)
 
 
 def shards(n, tokens, expert_ids, gates, gate_proj, up_proj, down_proj_t):
@@ -468,13 +465,13 @@
             vmem(up_proj.shape[1:], BF16),
             vmem((2, out_feats, down_proj_t.shape[2]), BF16),
             dma((7,)),
-            dma((2, n)), dma((2, n)),
-            dma((2, n)), dma((2, n)),
-            dma((2, cap, 2, top, CHUNKS)), dma((2, cap, 2, top, CHUNKS)),
-            dma((2, cap, n)), dma((2, cap, n)),
-            dma((2, cap, 2, top, n // 2)), dma((2, cap, 2, top, n // 2)),
-            dma((n,)), dma((n,)),
-            dma((n,)), dma((n,)),
+            dma((2,)), dma((2,)),
+            dma((2,)), dma((2, CHUNKS)),
+            dma((2, cap)), dma((2, cap, 2, top, CHUNKS)),
+            dma((2, cap)), dma((2, cap, n)),
+            dma((2, cap)), dma((2, cap, 2, top, n // 2)),
+            dma, dma,
+            dma, dma,
         ],
         compiler_params=pltpu.CompilerParams(collective_id=0, has_side_effects=True),
         name="experts",

time: 78.9 us -> 74.8 us (0.948)
  Pallas kernels: 77.3 us -> 73.2 us
    pallas_call x1, Pallas kernels: 77.3 us -> 73.2 us  [shards(): pl.pallas_call(functools.partial(kernel, n, cap), out_shape=jax.ShapeDtyp...]
where the time goes in v4:
time: 74.8 us; the launch traced here: 74.5 us
  Pallas kernels  73.2 us (98%)
  local copies, waits for them, and re-layouts  1.3 us (2%)
    pallas_call x1, Pallas kernels, shards(): pl.pallas_call(functools.partial(kernel, n, cap), out_shape=jax.ShapeDtyp...  73.2 us

profile of v4, /device:TPU:1, one launch (start us, length us, event | category | flops | bytes accessed | tf_op | source)
XLA Modules:
  0.0 74.5 jit_solution(7421587012049240165)
XLA Ops:
  0.0 73.2 %experts.1 = bf16[6,512]{1,0:T(8,128)(2,1)} custom-call(bf16[6,512]{1,0:T(8,128)(2,1)} %tok_hbm.1, s32[2,6]{1,0:T(2,128)} %bitcast.8, f32[2,6]{1,0:T(2,128)} %bitcast.9, bf16[4096,128]{1,0:T(8,128)(2,1)} %bitcast.5, bf16[4096,128]{1,0:T(8,128)(2,1)} %bitcast.6, bf16[64,8192]{1,0:T(8,128)(2,1)} %bitcast.7), custom_call_target="tpu_custom_call" | custom-call | tf_op jit(solution)/shard_map/experts/pallas_call | solution.py:443
  73.2 1.3 %copy.8 = bf16[6,512]{1,0:T(8,128)(2,1)} copy(bf16[6,512]{1,0:T(8,128)(2,1)} %experts.1) | data formatting | bytes 12288

commit v5 on v4

--- a/solution.py
+++ b/solution.py
@@ -13,7 +13,6 @@
 NARROW = ("shard_1", "shard_0")
 WIDE = ("shard_0", "shard_1")
 CHUNKS = 2
-LEAPS = (0, 1, 2)
 SPAN = 64
 F32, BF16 = jnp.float32, jnp.bfloat16
 
@@ -148,7 +147,7 @@
 
     def a3(h, s, way, k, j):
         step = 1 if way == 0 else -1
-        base = k - 1 if s not in LEAPS else (0 if k <= 2 else 2)
+        base = 0 if k <= 2 else 2
         unit = rows.at[h, s, plus(wid[h], -step * base), pl.ds(j * per, per)]
         return pltpu.make_async_remote_copy(
             src_ref=unit,
@@ -170,9 +169,14 @@
         for s in range(cap):
             for h in range(2):
                 for way in range(2):
-                    for k in (2, 1) if s in LEAPS else (1,):
-                        if k <= top and split(way, k, j, CHUNKS):
-                            a3(h, s, way, k, j).start()
+                    if top >= 2 and split(way, 2, j, CHUNKS):
+                        a3(h, s, way, 2, j).start()
+    for s in range(cap):
+        for j in range(CHUNKS):
+            for h in range(2):
+                for way in range(2):
+                    if split(way, 1, j, CHUNKS):
+                        a3(h, s, way, 1, j).start()
 
     def pass_rows(s, k):
         for j in range(CHUNKS):
@@ -180,8 +184,7 @@
                 for way in range(2):
                     if split(way, k, j, CHUNKS):
                         a3(h, s, way, k, j).wait_recv()
-                    after = (k + 1,) if s not in LEAPS else ((4, 3) if k == 2 else ())
-                    for later in after:
+                    for later in (4, 3) if k == 2 else ():
                         if later <= top and split(way, later, j, CHUNKS):
                             a3(h, s, way, later, j).start()
 
@@ -247,24 +250,15 @@
             for h in range(2):
                 c1(h, s, top).start()
 
-    slow = [s for s in range(cap) if s not in LEAPS]
-    quick = [s for s in range(cap) if s in LEAPS]
-    for k in range(1, top + 1):
-        for s in slow if k < top else ():
-            pass_rows(s, k)
-        if k == 2 or k == top == 1:
-            for s in quick:
-                for q in range(1, min(top, 2) + 1):
-                    pass_rows(s, q)
-        if k == min(3, top):
-            for copy in loads:
-                copy.wait()
-            for s in quick:
-                for q in range(3, top + 1):
-                    pass_rows(s, q)
-                begin(s)
-    for s in slow:
-        pass_rows(s, top)
+    if top >= 2:
+        for s in range(cap):
+            pass_rows(s, 2)
+    for copy in loads:
+        copy.wait()
+    for s in range(cap):
+        for k in (1, 3, 4):
+            if k <= top:
+                pass_rows(s, k)
         begin(s)
 
     acc[...] = jnp.zeros_like(acc)

time: 74.8 us -> 74.1 us (level)
  no operation moved by 1% of the time
where the time goes in v5:
time: 74.1 us; the launch traced here: 73.9 us
  Pallas kernels  72.6 us (98%)
  local copies, waits for them, and re-layouts  1.3 us (2%)
    pallas_call x1, Pallas kernels, shards(): pl.pallas_call(functools.partial(kernel, n, cap), out_shape=jax.ShapeDtyp...  72.6 us

profile of v5, /device:TPU:1, one launch (start us, length us, event | category | flops | bytes accessed | tf_op | source)
XLA Modules:
  0.0 73.9 jit_solution(7886252283542272424)
XLA Ops:
  0.0 72.6 %experts.1 = bf16[6,512]{1,0:T(8,128)(2,1)} custom-call(bf16[6,512]{1,0:T(8,128)(2,1)} %tok_hbm.1, s32[2,6]{1,0:T(2,128)} %bitcast.8, f32[2,6]{1,0:T(2,128)} %bitcast.9, bf16[4096,128]{1,0:T(8,128)(2,1)} %bitcast.5, bf16[4096,128]{1,0:T(8,128)(2,1)} %bitcast.6, bf16[64,8192]{1,0:T(8,128)(2,1)} %bitcast.7), custom_call_target="tpu_custom_call" | custom-call | tf_op jit(solution)/shard_map/experts/pallas_call | solution.py:437
  72.6 1.3 %copy.8 = bf16[6,512]{1,0:T(8,128)(2,1)} copy(bf16[6,512]{1,0:T(8,128)(2,1)} %experts.1) | data formatting | bytes 12288

commit v6 on v5

--- a/solution.py
+++ b/solution.py
@@ -21,7 +21,7 @@
     n, cap, tok_hbm, ids_hbm, gates_hbm, gate_hbm, up_hbm, down_hbm, out_ref,
     tok_v, ids_v, gates_v, stage, toks, sel, rows, part, hid, acc, give, got, got32, pass_on, back,
     gate_w, up_w, down_w,
-    load_sem, a1_send, a1_recv, a2_send, a2_recv, a3_send, a3_recv,
+    load_sem, a1_send, a1_recv, a2_send, a2_recv, a3_send, a3_recv, a3_rest,
     c1_send, c1_recv, c2_send, c2_recv, e1_send, e1_recv, e2_send, e2_recv,
 ):
     e = lax.axis_index("expert")
@@ -153,7 +153,7 @@
             src_ref=unit,
             dst_ref=unit,
             send_sem=a3_send.at[h, s],
-            recv_sem=a3_recv.at[h, s, way, k - 1, j],
+            recv_sem=a3_recv.at[h, s, way, j] if k == 2 else a3_rest.at[h, s],
             device_id={WIDE[h]: plus(wid[h], step * (k - base))},
             device_id_type=MESH,
         )
@@ -178,13 +178,13 @@
                     if split(way, 1, j, CHUNKS):
                         a3(h, s, way, 1, j).start()
 
-    def pass_rows(s, k):
+    def pass_rows(s):
         for j in range(CHUNKS):
             for h in range(2):
                 for way in range(2):
-                    if split(way, k, j, CHUNKS):
-                        a3(h, s, way, k, j).wait_recv()
-                    for later in (4, 3) if k == 2 else ():
+                    if split(way, 2, j, CHUNKS):
+                        a3(h, s, way, 2, j).wait_recv()
+                    for later in (4, 3):
                         if later <= top and split(way, later, j, CHUNKS):
                             a3(h, s, way, later, j).start()
 
@@ -200,7 +200,7 @@
             src_ref=hid.at[h, s, wid[h], place[send]],
             dst_ref=hid.at[h, s, wid[h], place[d]],
             send_sem=c1_send.at[h, s],
-            recv_sem=c1_recv.at[h, s, d],
+            recv_sem=c1_recv.at[h, s, pairs if d == top else place[d] // 2],
             device_id={NARROW[h]: plus(nar[h], to)},
             device_id_type=MESH,
         )
@@ -252,13 +252,13 @@
 
     if top >= 2:
         for s in range(cap):
-            pass_rows(s, 2)
+            pass_rows(s)
     for copy in loads:
         copy.wait()
     for s in range(cap):
-        for k in (1, 3, 4):
-            if k <= top:
-                pass_rows(s, k)
+        for h in range(2):
+            units = n - 1 - (2 if top > 2 else 1 if top == 2 else 0)
+            bytes_of(rows.at[h, s, pl.ds(0, units)], a3_rest.at[h, s])
         begin(s)
 
     acc[...] = jnp.zeros_like(acc)
@@ -306,12 +306,14 @@
                 c2(h, s, way, k + 1, i).start()
 
     for s in range(cap):
-        for h in range(2):
-            for p in range(1, n - 1):
-                c1(h, s, order[p]).wait_recv()
-                if p % 2 == 1:
-                    launch(h, s, p // 2)
-                if top > 1 and order[p] == (top - 1 if s % 2 == 0 else n - top + 1):
+        for i in range(pairs):
+            for h in range(2):
+                count = sum(1 for p in (2 * i, 2 * i + 1) if order[p] not in (0, top))
+                if count:
+                    bytes_of(hid.at[h, s, 0, pl.ds(0, count)], c1_recv.at[h, s, i])
+                if i < early:
+                    launch(h, s, i)
+                if top > 1 and place[top - 1 if s % 2 == 0 else n - top + 1] // 2 == i:
                     c1(h, s, top).start()
     for t in range(1, top + 2):
         if t == top + 1:
@@ -461,8 +463,8 @@
             dma((7,)),
             dma((2,)), dma((2,)),
             dma((2,)), dma((2, CHUNKS)),
-            dma((2, cap)), dma((2, cap, 2, top, CHUNKS)),
-            dma((2, cap)), dma((2, cap, n)),
+            dma((2, cap)), dma((2, cap, 2, CHUNKS)), dma((2, cap)),
+            dma((2, cap)), dma((2, cap, n // 2 + 1)),
             dma((2, cap)), dma((2, cap, 2, top, n // 2)),
             dma, dma,
             dma, dma,

time: 74.1 us -> 73.3 us (0.989)
  Pallas kernels: 72.6 us -> 71.8 us
    pallas_call x1, Pallas kernels: 72.6 us -> 71.8 us  [shards(): pl.pallas_call(functools.partial(kernel, n, cap), out_shape=jax.ShapeDtyp...]
where the time goes in v6:
time: 73.3 us; the launch traced here: 73.1 us
  Pallas kernels  71.8 us (98%)
  local copies, waits for them, and re-layouts  1.3 us (2%)
    pallas_call x1, Pallas kernels, shards(): pl.pallas_call(functools.partial(kernel, n, cap), out_shape=jax.ShapeDtyp...  71.8 us

profile of v6, /device:TPU:1, one launch (start us, length us, event | category | flops | bytes accessed | tf_op | source)
XLA Modules:
  0.0 73.1 jit_solution(14749294216470889178)
XLA Ops:
  0.0 71.8 %experts.1 = bf16[6,512]{1,0:T(8,128)(2,1)} custom-call(bf16[6,512]{1,0:T(8,128)(2,1)} %tok_hbm.1, s32[2,6]{1,0:T(2,128)} %bitcast.8, f32[2,6]{1,0:T(2,128)} %bitcast.9, bf16[4096,128]{1,0:T(8,128)(2,1)} %bitcast.5, bf16[4096,128]{1,0:T(8,128)(2,1)} %bitcast.6, bf16[64,8192]{1,0:T(8,128)(2,1)} %bitcast.7), custom_call_target="tpu_custom_call" | custom-call | tf_op jit(solution)/shard_map/experts/pallas_call | solution.py:439
  71.8 1.3 %copy.8 = bf16[6,512]{1,0:T(8,128)(2,1)} copy(bf16[6,512]{1,0:T(8,128)(2,1)} %experts.1) | data formatting | bytes 12288
